TPU v7x, 512 devices: a whole 4x8x8 slice. The times are simulated.
512 devices in a mesh: dp: 16 (over y_lo, x), space: 32 (over z, y_hi, core).
Axes of the slice: x: 4, y: 8 (y_hi: 2, y_lo: 4; y = y_hi * 4 + y_lo), z: 8, core: 2. Of those that a mesh axis runs over, the one named last changes fastest.
Arguments:
- fields: bfloat16 [16, 100, 131072], P('dp', None, 'space'), may hold values from -6 to 6
- cell_index: int32 [1024, 128], P('space'), may hold values from 0 to 6143
- interp_weight: bfloat16 [1024, 16, 128], P('space'), may hold values from 0 to 2, as said below
- w_in: bfloat16 [100, 1024], replicated, may hold values from -0.625 to 0.625
- ln_gain: float32 [1024], replicated, may hold values from 0.5 to 1.5
- w_qkv: bfloat16 [1024, 3072], P('dp'), may hold values from -0.1875 to 0.1875
- w_out: bfloat16 [1024, 1024], P('dp'), may hold values from -3 to 3
Outputs:
- latent: bfloat16 [16, 16384, 1024], P('dp', 'space')
- update: bfloat16 [16, 16384, 1024], P('dp', 'space')
Inputs may be any that keep to these rules, and one draw needn't show every extreme that they name: `interp_weight`: in each block the slots from some count on carry zero weight for all its 16 nodes; that count lies between 48 and 128. `cell_index`: indexes a shard's 4096 cells extended by 1024 cells of each neighbouring shard, lower neighbour first.
All inputs are finite; a program needn't handle non-finite values.
Results may differ from a plain program's by a relative error of at most 0.0068.
Values may be sent and summed in bfloat16 or wider, within the bound.
A program may use at most 128 MiB of HBM per device.

v0:
```python
import math

import jax
import jax.numpy as jnp
from jax import lax
from jax.sharding import PartitionSpec as P

HEADS = 16


def padded(array, sides, width):
    for axis, dim in sides:
        size, length = (lax.axis_size(axis), array.shape[dim])
        up = [(i, (i + 1) % size) for i in range(size)]
        down = [(j, i) for i, j in up]
        last = lax.slice_in_dim(array, length - width, length, axis=dim)
        first = lax.slice_in_dim(array, 0, width, axis=dim)
        before = lax.ppermute(last, axis, up)
        after = lax.ppermute(first, axis, down)
        array = jnp.concatenate([before, array, after], axis=dim)
    return array


def unit_heads(projected):
    head_size = projected.shape[1] // HEADS
    head_rows = projected.reshape(projected.shape[0], HEADS, head_size)
    scale_rows = jnp.sqrt(jnp.mean(head_rows * head_rows, axis=-1, keepdims=True) + 1e-06)
    return (head_rows / scale_rows).astype(jnp.bfloat16).reshape(projected.shape)


def shards(fields, cell_index, interp_weight, w_in, ln_gain, w_qkv, w_out):
    width = w_qkv.shape[1] // 3
    full_qkv, full_out = (
        lax.all_gather(w_qkv, "dp", axis=0, tiled=True),
        lax.all_gather(w_out, "dp", axis=0, tiled=True),
    )
    grid_field = fields[0]
    cell_count = grid_field.shape[1]
    cell_reach = cell_count // 4
    extended = padded(grid_field, (("space", 1),), cell_reach)
    picked = jnp.take(extended, cell_index, axis=1)
    encoded = jnp.einsum("cbs,bns->bnc", picked, interp_weight, preferred_element_type=jnp.float32)
    node_count = encoded.shape[0] * encoded.shape[1]
    encoded = encoded.reshape(node_count, encoded.shape[2]).astype(jnp.bfloat16)
    embedded = jnp.dot(encoded, w_in, preferred_element_type=jnp.float32)
    average = jnp.mean(embedded, axis=1, keepdims=True)
    centered = embedded - average
    spread = jnp.mean(centered * centered, axis=1, keepdims=True)
    normed = (centered / jnp.sqrt(spread + 1e-05) * ln_gain).astype(jnp.bfloat16)
    margin = node_count // 2
    bordered = padded(normed, (("space", 0),), margin)
    side_normed = jnp.concatenate([bordered[:margin], bordered[margin + node_count :]], axis=0)
    projected = jnp.dot(normed, full_qkv, preferred_element_type=jnp.float32)
    side_projected = jnp.dot(side_normed, full_qkv[:, width:], preferred_element_type=jnp.float32)
    queries = unit_heads(projected[:, :width])
    own_pairs = jnp.concatenate(
        [
            unit_heads(projected[:, width : 2 * width]),
            projected[:, 2 * width :].astype(jnp.bfloat16),
        ],
        axis=1,
    )
    side_pairs = jnp.concatenate(
        [unit_heads(side_projected[:, :width]), side_projected[:, width:].astype(jnp.bfloat16)],
        axis=1,
    )
    window = jnp.concatenate([side_pairs[:margin], own_pairs, side_pairs[margin:]], axis=0)
    head_size = width // HEADS
    group_width = 2 * head_size

    def attend(group_index):
        offset = group_index * group_width
        query_group = lax.dynamic_slice_in_dim(queries, offset, group_width, 1).reshape(
            node_count, 2, head_size
        )
        key_group = lax.dynamic_slice_in_dim(window, offset, group_width, 1).reshape(
            window.shape[0], 2, head_size
        )
        value_group = lax.dynamic_slice_in_dim(window, width + offset, group_width, 1).reshape(
            window.shape[0], 2, head_size
        )
        scores = jnp.einsum(
            "qhd,khd->hqk", query_group, key_group, preferred_element_type=jnp.float32
        ) / math.sqrt(head_size)
        weights = jnp.exp(scores)
        probs = (weights / jnp.sum(weights, axis=2, keepdims=True)).astype(jnp.bfloat16)
        mixed_rows = jnp.einsum(
            "hqk,khd->qhd", probs, value_group, preferred_element_type=jnp.float32
        )
        return mixed_rows.astype(jnp.bfloat16).reshape(node_count, group_width)

    grouped = lax.map(attend, jnp.arange(HEADS // 2, dtype=jnp.int32))
    attended = grouped.transpose(1, 0, 2).reshape(node_count, width)
    update = jnp.dot(attended, full_out, preferred_element_type=jnp.float32)
    return (embedded.astype(jnp.bfloat16)[None], update.astype(jnp.bfloat16)[None])


def solution(mesh):
    placed = (
        P("dp", None, "space"),
        P("space", None),
        P("space", None, None),
        P(),
        P(),
        P("dp", None),
        P("dp", None),
    )
    return jax.shard_map(
        shards,
        mesh=mesh,
        in_specs=placed,
        out_specs=(P("dp", "space", None), P("dp", "space", None)),
        check_vma=False,
    )
```

profile of v0, /device:TPU:192, one launch (start us, length us, event | category | flops | bytes accessed | tf_op | source)
XLA Modules:
  0.0 249.3 jit_solution(16279916706704496909)
XLA Ops:
  8.0 1.6 copy.13
  9.6 6.3 %collective-permute-start.1 = (bf16[100,1024]{0,1:T(8,128)(2,1)S(1)}, bf16[100,1024]{0,1:T(8,128)(2,1)S(1)}, u32[]{:S(2)}, u32[]{:S(2)}) collective-permute-start(bf16[100,1024]{0,1:T(8,128)(2,1)S(1)} %get-tuple-element.101), channel_id=1, source_target_pairs={{1,0},{2,1},{3,2},{4,3},{5,4},{6,5},{7,6},{8,7},{9,8},{10,9},{11,1... | collective-permute-start | bytes 614408 | tf_op jit(solution)/shard_map/ppermute | solution.py:19
  15.9 1.9 collective-permute-start
  17.9 2.6 %collective-permute-done.1 = bf16[100,1024]{0,1:T(8,128)(2,1)S(1)} collective-permute-done((bf16[100,1024]{0,1:T(8,128)(2,1)S(1)}, bf16[100,1024]{0,1:T(8,128)(2,1)S(1)}, u32[]{:S(2)}, u32[]{:S(2)}) %collective-permute-start.1) | collective-permute-done | bytes 204832 | tf_op jit(solution)/shard_map/ppermute | solution.py:19
  20.4 11.5 %collective-permute-done = bf16[100,1024]{0,1:T(8,128)(2,1)S(1)} collective-permute-done((bf16[100,1024]{0,1:T(8,128)(2,1)S(1)}, bf16[100,1024]{0,1:T(8,128)(2,1)S(1)}, u32[]{:S(2)}, u32[]{:S(2)}) %collective-permute-start) | collective-permute-done | bytes 204832 | tf_op jit(solution)/shard_map/ppermute | solution.py:18
  32.3 12.1 %gather_fusion = bf16[4096,100]{1,0:T(8,128)(2,1)S(1)} fusion(bf16[100,6144]{0,1:T(8,128)(2,1)S(1)} %pad_maximum_fusion, s32[4096]{0:T(1024)S(1)} %bitcast_clamp_fusion), kind=kCustom, calls=%fused_computation | custom fusion | bytes 1654784 | tf_op jit(solution)/shard_map/jit(_take)/gather | solution.py:41
  49.1 1.9 collective-permute-start.3
  51.0 2.6 %collective-permute-start.2 = (bf16[256,1024]{1,0:T(8,128)(2,1)S(1)}, bf16[256,1024]{1,0:T(8,128)(2,1)S(1)}, u32[]{:S(2)}, u32[]{:S(2)}) collective-permute-start(bf16[256,1024]{1,0:T(8,128)(2,1)S(1)} %get-tuple-element.98), channel_id=1, source_target_pairs={{0,1},{1,2},{2,3},{3,4},{4,5},{5,6},{6,7},{7,8},{8,9},{9,10},{10,1... | collective-permute-start | bytes 1572872 | tf_op jit(solution)/shard_map/ppermute | solution.py:18
  53.7 19.1 %collective-permute-done.3 = bf16[256,1024]{1,0:T(8,128)(2,1)S(1)} collective-permute-done((bf16[256,1024]{1,0:T(8,128)(2,1)S(1)}, bf16[256,1024]{1,0:T(8,128)(2,1)S(1)}, u32[]{:S(2)}, u32[]{:S(2)}) %collective-permute-start.3) | collective-permute-done | bytes 524320 | tf_op jit(solution)/shard_map/ppermute | solution.py:19
  72.8 9.2 %collective-permute-done.2 = bf16[256,1024]{1,0:T(8,128)(2,1)S(1)} collective-permute-done((bf16[256,1024]{1,0:T(8,128)(2,1)S(1)}, bf16[256,1024]{1,0:T(8,128)(2,1)S(1)}, u32[]{:S(2)}, u32[]{:S(2)}) %collective-permute-start.2) | collective-permute-done | bytes 524320 | tf_op jit(solution)/shard_map/ppermute | solution.py:18
  82.0 45.4 %all-gather.3.cloned.1.call-done = bf16[1024,3072]{1,0:T(8,128)(2,1)} async-done(((bf16[64,3072]{1,0:T(8,128)(2,1)}), bf16[1024,3072]{1,0:T(8,128)(2,1)}) %all-gather.3.cloned.1.call-update) | async-done | bytes 6291472 | tf_op jit(solution)/shard_map/all_gather | solution.py:34
  127.4 4.7 %fusion.8 = f32[512,2048]{1,0:T(8,128)S(1)} fusion(bf16[1024,3072]{1,0:T(8,128)(2,1)} %all-gather.3.cloned.1.call-done, bf16[256,1024]{1,0:T(8,128)(2,1)S(1)} %collective-permute-done.3, bf16[256,1024]{1,0:T(8,128)(2,1)S(1)} %collective-permute-done.2), kind=kOutput, calls=%fused_computation.16 | convolution fusion | flops 2149580800 | bytes 9437184 | tf_op jit(solution)/shard_map/dot_general | solution.py:54
  132.3 1.9 copy-done.3
  135.4 3.4 %fusion.24 = f32[512,3072]{1,0:T(8,128)S(1)} fusion(bf16[512,1024]{1,0:T(8,128)(2,1)S(1)} %copy-done.6, bf16[1024,3072]{1,0:T(8,128)(2,1)S(1)} %copy-done.10), kind=kOutput, calls=%fused_computation.59 | convolution fusion | flops 3221225472 | bytes 13631488 | tf_op jit(solution)/shard_map/dot_general | solution.py:53
  140.1 1.7 copy-done.2
  141.7 2.4 slice_multiply_fusion
  144.2 1.8 copy.15
  146.0 1.9 bitcast_reduce_fusion.2
  148.2 1.8 copy.16
  150.0 2.6 %divide_convert_fusion.6 = bf16[512,1024]{1,0:T(8,128)(2,1)S(1)} fusion(f32[512,1024]{1,0:T(8,128)} %copy.16, f32[512,2048]{1,0:T(8,128)} %copy-done.3), kind=kLoop, calls=%fused_computation.27 | loop fusion | flops 1048576 | bytes 5242880 | tf_op jit(solution)/shard_map/convert_element_type | solution.py:28
  152.6 2.9 %copy.19 = f32[512,1024]{0,1:T(8,128)} copy(f32[512,1024]{1,0:T(8,128)} %get-tuple-element.94) | data formatting | bytes 4194304 | tf_op jit(solution)/shard_map/mul | solution.py:27
  155.6 1.9 bitcast_reduce_fusion
  157.5 1.6 div.86
  159.1 2.9 %copy.20 = f32[512,1024]{1,0:T(8,128)} copy(f32[512,1024]{0,1:T(8,128)} %bitcast.62) | data formatting | bytes 4194304 | tf_op jit(solution)/shard_map/div | solution.py:28
  162.0 2.9 %copy.17 = f32[512,1024]{0,1:T(8,128)} copy(f32[512,1024]{1,0:T(8,128)} %get-tuple-element.95) | data formatting | bytes 4194304 | tf_op jit(solution)/shard_map/mul | solution.py:27
  165.0 1.9 bitcast_reduce_fusion.1
  168.5 2.9 %copy.18 = f32[512,1024]{1,0:T(8,128)} copy(f32[512,1024]{0,1:T(8,128)} %bitcast.63) | data formatting | bytes 4194304 | tf_op jit(solution)/shard_map/div | solution.py:28
  171.4 4.4 %divide_convert_fusion.4 = (bf16[512,1024]{1,0:T(8,128)(2,1)S(1)}, bf16[512,1024]{1,0:T(8,128)(2,1)S(1)}) fusion(f32[512,1024]{1,0:T(8,128)} %copy.20, f32[512,3072]{1,0:T(8,128)} %copy-done.2, f32[512,1024]{1,0:T(8,128)} %copy.18), kind=kLoop, calls=%fused_computation.25 | loop fusion | flops 2097152 | bytes 10485760 | tf_op jit(solution)/shard_map/convert_element_type | solution.py:28
  177.0 20.1 %fusion.7 = bf16[1024,2048]{1,0:T(8,128)(2,1)} fusion(bf16[512,1024]{1,0:T(8,128)(2,1)S(1)} %slice.81, bf16[512,1024]{1,0:T(8,128)(2,1)S(1)} %divide_convert_fusion.6, bf16[512,1024]{1,0:T(8,128)(2,1)S(1)} %copy-done.4, bf16[512,1024]{1,0:T(8,128)(2,1)S(1)} %get-tuple-element.93, bf16[256,2048]{1,0:T(8,128)(2,1)S(1)} %fusion.11), kind=kLoop, calls=%fused_computation.15 | loop fusion | flops 27262976 | bytes 9437184 | tf_op jit(solution)/shard_map/concatenate | solution.py:67
  197.1 6.5 %copy.21 = bf16[1024,2048]{0,1:T(8,128)(2,1)} copy(bf16[1024,2048]{1,0:T(8,128)(2,1)} %fusion.7) | data formatting | bytes 8388608 | tf_op jit(solution)/shard_map/while | solution.py:92
  203.6 34.9 %while.12 = (s32[]{:T(128)}, bf16[8,512,128]{1,2,0:T(8,128)(2,1)S(1)}, s32[8]{0:T(128)S(1)}, bf16[1024,2048]{0,1:T(8,128)(2,1)}, bf16[512,1024]{1,0:T(8,128)(2,1...) while((s32[]{:T(128)}, ...), condition=%wide.region_7.8_spmd, body=%wide.region_5.7_spmd.sunk | while | flops 273742848 | bytes 11018490 | solution.py:92
  238.6 3.9 %fusion.10 = bf16[1,512,1024]{2,1,0:T(8,128)(2,1)} fusion(bf16[512,1024]{0,1:T(8,128)(2,1)S(1)} %bitcast.69, bf16[1024,1024]{1,0:T(8,128)(2,1)} %all-gather.5.cloned.1.call-done), kind=kOutput, calls=%fused_computation.35 | convolution fusion | flops 1074266112 | bytes 4194304 | tf_op jit(solution)/shard_map/dot_general | solution.py:94
  (106 shorter events, 40.8 us)
Async XLA Ops:
  7.2 38.5 %copy-start = (bf16[100,1024]{1,0:T(8,128)(2,1)S(1)}, bf16[100,1024]{1,0:T(8,128)(2,1)}, u32[]{:S(2)}) copy-start(bf16[100,1024]{1,0:T(8,128)(2,1)} %param.12) | copy-start | bytes 614404
  7.2 10.7 %copy-start.8 = (s32[32,128]{1,0:T(8,128)S(1)}, s32[32,128]{1,0:T(8,128)}, u32[]{:S(2)}) copy-start(s32[32,128]{1,0:T(8,128)} %param.10) | copy-start | bytes 49156
  7.2 120.2 %all-gather.3.cloned.1.call-start = ((), (), s32[]{:S(2)}) async-start(), calls=%async_computation | async-start | bytes 6684672 | tf_op jit(solution)/shard_map/all_gather | solution.py:34
  7.9 230.7 %all-gather.5.cloned.1.call-start = ((), (), s32[]{:S(2)}) async-start(), calls=%async_computation.1 | async-start | bytes 2228224 | tf_op jit(solution)/shard_map/all_gather | solution.py:35
  9.6 10.8 %collective-permute-start.1 = (bf16[100,1024]{0,1:T(8,128)(2,1)S(1)}, bf16[100,1024]{0,1:T(8,128)(2,1)S(1)}, u32[]{:S(2)}, u32[]{:S(2)}) collective-permute-start(bf16[100,1024]{0,1:T(8,128)(2,1)S(1)} %get-tuple-element.101), channel_id=1, source_target_pairs={{1,0},{2,1},{3,2},{4,3},{5,4},{6,5},{7,6},{8,7},{9,8},{10,9},{11,1... | collective-permute-start | bytes 614408 | tf_op jit(solution)/shard_map/ppermute | solution.py:19
  15.9 16.0 %collective-permute-start = (bf16[100,1024]{0,1:T(8,128)(2,1)S(1)}, bf16[100,1024]{0,1:T(8,128)(2,1)S(1)}, u32[]{:S(2)}, u32[]{:S(2)}) collective-permute-start(bf16[100,1024]{0,1:T(8,128)(2,1)S(1)} %get-tuple-element.100), channel_id=1, source_target_pairs={{0,1},{1,2},{2,3},{3,4},{4,5},{5,6},{6,7},{7,8},{8,9},{9,10},{10,1... | collective-permute-start | bytes 614408 | tf_op jit(solution)/shard_map/ppermute | solution.py:18
  32.2 12.8 %copy-start.11 = (bf16[32,16,128]{2,1,0:T(8,128)(2,1)S(1)}, bf16[32,16,128]{2,1,0:T(8,128)(2,1)}, u32[]{:S(2)}) copy-start(bf16[32,16,128]{2,1,0:T(8,128)(2,1)} %param.11) | copy-start | bytes 393220
  45.6 0.9 copy-start.9
  48.0 1.1 copy-start.5
  49.1 23.7 %collective-permute-start.3 = (bf16[256,1024]{1,0:T(8,128)(2,1)S(1)}, bf16[256,1024]{1,0:T(8,128)(2,1)S(1)}, u32[]{:S(2)}, u32[]{:S(2)}) collective-permute-start(bf16[256,1024]{1,0:T(8,128)(2,1)S(1)} %get-tuple-element.99), channel_id=1, source_target_pairs={{1,0},{2,1},{3,2},{4,3},{5,4},{6,5},{7,6},{8,7},{9,8},{10,9},{11,1... | collective-permute-start | bytes 1572872 | tf_op jit(solution)/shard_map/ppermute | solution.py:19
  51.0 30.9 %collective-permute-start.2 = (bf16[256,1024]{1,0:T(8,128)(2,1)S(1)}, bf16[256,1024]{1,0:T(8,128)(2,1)S(1)}, u32[]{:S(2)}, u32[]{:S(2)}) collective-permute-start(bf16[256,1024]{1,0:T(8,128)(2,1)S(1)} %get-tuple-element.98), channel_id=1, source_target_pairs={{0,1},{1,2},{2,3},{3,4},{4,5},{5,6},{6,7},{7,8},{8,9},{9,10},{10,1... | collective-permute-start | bytes 1572872 | tf_op jit(solution)/shard_map/ppermute | solution.py:18
  127.4 6.9 %copy-start.10 = (bf16[1024,3072]{1,0:T(8,128)(2,1)S(1)}, bf16[1024,3072]{1,0:T(8,128)(2,1)}, u32[]{:S(2)}) copy-start(bf16[1024,3072]{1,0:T(8,128)(2,1)} %all-gather.3.cloned.1.call-done) | copy-start | bytes 18874372
  132.1 2.0 copy-start.3
  134.1 1.2 copy-start.6
  138.8 3.0 %copy-start.2 = (f32[512,3072]{1,0:T(8,128)}, f32[512,3072]{1,0:T(8,128)S(1)}, u32[]{:S(2)}) copy-start(f32[512,3072]{1,0:T(8,128)S(1)} %fusion.24) | copy-start | bytes 18874372
  175.8 1.2 copy-start.4
  197.1 6.5 %copy-start.7 = (bf16[8,512,128]{1,2,0:T(8,128)(2,1)S(1)}, bf16[8,512,128]{1,2,0:T(8,128)(2,1)}, u32[]{:S(2)}) copy-start(bf16[8,512,128]{1,2,0:T(8,128)(2,1)} %custom-call.2) | copy-start | bytes 3145732
  238.6 3.9 %copy-start.1 = (bf16[100,1024]{1,0:T(8,128)(2,1)S(1)}, bf16[100,1024]{1,0:T(8,128)(2,1)}, u32[]{:S(2)}) copy-start(bf16[100,1024]{1,0:T(8,128)(2,1)} %param.12) | copy-start | bytes 614404
Sparse Core Ops, SparseCore 0:
  10.1 117.3 all-gather.2
  129.5 84.1 all-gather.4
where the time goes:
time: 251 us; the launch traced here: 249 us
  waiting for transfers between devices  88.5 us (35%)
  local copies, waits for them, and re-layouts  62.8 us (25%)
  other arithmetic  37.6 us (15%)
  matrix products  27.6 us (11%)
  between operations  14.4 us (6%)
  starting transfers between devices  12.8 us (5%)
  loops' own time  5.76 us (2%)
    all_gather x1, waiting for transfers between devices, shards(): lax.all_gather(w_qkv, 'dp', axis=0, tiled=True)  45.4 us
    ppermute x2, waiting for transfers between devices, padded(): after = lax.ppermute(first, axis, down)  21.7 us
    ppermute x2, waiting for transfers between devices, padded(): before = lax.ppermute(last, axis, up)  20.7 us
    concatenate x1, other arithmetic, shards(): jnp.concatenate([side_pairs[:margin], own_pairs, side_pairs[margin:]], ax...  20.1 us
    gather x2, local copies, waits for them, and re-layouts, shards(): picked = jnp.take(extended, cell_index, axis=1)  12.8 us
    div x6, local copies, waits for them, and re-layouts, unit_heads(): head_rows / scale_rows  11.2 us
    dynamic_slice x8, local copies, waits for them, and re-layouts, attend(): lax.dynamic_slice_in_dim(window, offset, group_width, 1)  8.56 us
    unnamed x25, local copies, waits for them, and re-layouts  8.43 us
  transfers between devices with their start and end apart: 6, of which 5 were waited for; matrix products, arithmetic and copies ran while one was open for 47% of the time, Pallas kernels for 0%

commit v1 on v0

v1 whole, which is shorter than its diff:
```python
import functools
import math

import jax
import jax.numpy as jnp
from jax import lax
from jax.experimental import pallas as pl
from jax.experimental.pallas import tpu as pltpu
from jax.sharding import PartitionSpec as P

HEADS = 16
CH = 100
HALO_C = 1024
HALO_N = 256
NODE = 512
BLK = 32
CELL = 4096
REACH = CELL + 2 * HALO_C
LANES = 128
MESH = pl.DeviceIdType.MESH
PARTS = (("x", 1), ("x", -1), ("y", 1), ("y", -1))
RELATIVE = (0, -1, 1, 2)
ROWS = 32


def comm_kernel(
    fields, index, weight, w_qkv, w_out,
    enc_out, w_all,
    ext, ext_t, picked, enc, full,
    local_sem, cell_send, cell_recv, enc_send, enc_recv,
    send_sem, recv_sem, pair_send, pair_recv, store_sem,
):
    dp = lax.axis_index("dp")
    sp = lax.axis_index("space")
    x, y = dp % 4, dp // 4
    core, side, z = sp % 2, (sp // 2) % 2, sp // 4

    def at(new_y, new_x, new_side, new_core):
        return (new_y * 4 + new_x, z * 4 + new_side * 2 + new_core)

    up_side = (side + (y + 1) // 4) % 2
    down_side = (side + 1 - (y + 3) // 4) % 2
    step_to = {
        ("x", 1): at(y, (x + 1) % 4, side, core),
        ("x", -1): at(y, (x + 3) % 4, side, core),
        ("y", 1): at((y + 1) % 4, x, up_side, core),
        ("y", -1): at((y + 3) % 4, x, down_side, core),
    }
    partner = at(y, x, side, 1 - core)
    left = (dp, (sp + 31) % 32)
    right = (dp, (sp + 1) % 32)
    far = (dp, (sp + 31 + 2 * core) % 32)

    def rows_of(piece_y, piece_x, half):
        return pl.ds(pl.multiple_of((piece_y * 4 + piece_x) * 64 + half * ROWS, ROWS), ROWS)

    def shard(part):
        if part < 3:
            return w_qkv.at[:, pl.ds(part * 1024, 1024)]
        return w_out

    own_cells = pltpu.make_async_copy(fields, ext.at[:, pl.ds(HALO_C, CELL)], local_sem.at[0])
    own_cells.start()
    own_rows = [
        pltpu.make_async_copy(
            shard(part),
            full.at[part, pl.ds(pl.multiple_of(dp * 64, 64), 64)],
            local_sem.at[1 + part],
        )
        for part in range(4)
    ]
    for copy in own_rows:
        copy.start()

    barrier = pltpu.get_barrier_semaphore()
    for other in list(step_to.values()) + [partner, far]:
        pl.semaphore_signal(barrier, inc=1, device_id=other, device_id_type=MESH)
    pl.semaphore_wait(barrier, 6)

    sent = []

    def remote(src, dst, s_sem, r_sem, target):
        copy = pltpu.make_async_remote_copy(
            src_ref=src, dst_ref=dst, send_sem=s_sem, recv_sem=r_sem,
            device_id=target, device_id_type=MESH,
        )
        copy.start()
        sent.append(copy)
        return copy

    cells_right = remote(
        fields.at[:, pl.ds(CELL - HALO_C, HALO_C)], ext.at[:, pl.ds(0, HALO_C)],
        cell_send.at[0], cell_recv.at[0], right)
    cells_left = remote(
        fields.at[:, pl.ds(0, HALO_C)], ext.at[:, pl.ds(HALO_C + CELL, HALO_C)],
        cell_send.at[1], cell_recv.at[1], left)

    def origin(part, first, second):
        axis = PARTS[part][0]
        if axis == "x":
            return (y + 4 + second) % 4, (x + 4 + first) % 4
        return (y + 4 + first) % 4, (x + 4 + second) % 4

    def slot(first_at, kind):
        return first_at * 3 + kind

    copies = {}

    def move(part, first, second, direction_axis, direction, number):
        piece = origin(part, first, second)
        rows = rows_of(*piece, core)
        if first == 0 and second == 0:
            source = shard(part).at[pl.ds(pl.multiple_of(core * ROWS, ROWS), ROWS)]
        else:
            source = full.at[part, rows]
        copies[part, number] = remote(
            source, full.at[part, rows],
            send_sem.at[part * 15 + number], recv_sem.at[part * 15 + number],
            step_to[direction_axis, direction])

    pairs = {}

    def arrived(part, first, second, number):
        rows = rows_of(*origin(part, first, second), core)
        copies[part, number].wait_recv()
        pairs[part, number] = remote(
            full.at[part, rows], full.at[part, rows],
            pair_send.at[part * 15 + number], pair_recv.at[part * 15 + number], partner)

    def other_axis(part):
        return "y" if PARTS[part][0] == "x" else "x"

    for part, (axis, hand) in enumerate(PARTS):
        move(part, 0, 0, axis, 1, 0)
        move(part, 0, 0, axis, -1, 1)
    for part, (axis, hand) in enumerate(PARTS):
        move(part, 0, 0, other_axis(part), 1, 3 + slot(0, 0))
        move(part, 0, 0, other_axis(part), -1, 3 + slot(0, 1))

    def second_axis_out(part, first_at):
        first = RELATIVE[first_at]
        move(part, first, 0, other_axis(part), 1, 3 + slot(first_at, 0))
        move(part, first, 0, other_axis(part), -1, 3 + slot(first_at, 1))

    def turn(start, count):
        @pl.loop(0, count)
        def _(i):
            at_cell = pl.multiple_of(start + i * LANES, LANES)
            ext_t[pl.ds(at_cell, LANES), 0:CH] = ext[:, pl.ds(at_cell, LANES)].astype(jnp.float32).T

    own_cells.wait()
    turn(HALO_C, CELL // LANES)

    def stage_one():
        for part, (axis, hand) in enumerate(PARTS):
            arrived(part, -1, 0, 0)
            if hand == 1:
                move(part, -1, 0, axis, 1, 2)
            second_axis_out(part, 1)
            arrived(part, 1, 0, 1)
            if hand == -1:
                move(part, 1, 0, axis, -1, 2)
            second_axis_out(part, 2)

    def stage_two():
        for part in range(4):
            arrived(part, 2, 0, 2)
            second_axis_out(part, 3)

    def stage_three(first_at):
        first = RELATIVE[first_at]
        for part, (axis, hand) in enumerate(PARTS):
            arrived(part, first, -1, 3 + slot(first_at, 0))
            if hand == 1:
                move(part, first, -1, other_axis(part), 1, 3 + slot(first_at, 2))
            arrived(part, first, 1, 3 + slot(first_at, 1))
            if hand == -1:
                move(part, first, 1, other_axis(part), -1, 3 + slot(first_at, 2))

    def stage_four(first_at):
        for part in range(4):
            arrived(part, RELATIVE[first_at], 2, 3 + slot(first_at, 2))

    def encode(first_block, count):
        @pl.loop(first_block, first_block + count)
        def _(b):
            @pl.loop(0, LANES // 16)
            def _(group):
                for k in range(16):
                    j = group * 16 + k
                    picked[pl.ds(b * LANES + j, 1), :] = ext_t[pl.ds(index[b, j], 1), :]
        @pl.loop(first_block, first_block + count)
        def _(b):
            rows = picked[pl.ds(pl.multiple_of(b * LANES, LANES), LANES), :].astype(jnp.bfloat16)
            mixed = jnp.dot(weight[b], rows, preferred_element_type=jnp.float32)
            lane = lax.broadcasted_iota(jnp.int32, mixed.shape, 1)
            enc[pl.ds(pl.multiple_of(b * 16, 16), 16), :] = jnp.where(lane < CH, mixed, 0.0).astype(jnp.bfloat16)

    stage_one()
    cells_right.wait_recv()
    cells_left.wait_recv()
    turn(0, HALO_C // LANES)
    turn(HALO_C + CELL, HALO_C // LANES)
    stage_two()
    encode(0, 8)
    stage_three(0)
    encode(8, 8)
    enc_left = remote(
        enc.at[pl.ds(0, HALO_N)], enc.at[pl.ds(NODE + HALO_N, HALO_N)],
        enc_send.at[0], enc_recv.at[0], left)
    stage_three(1)
    encode(16, 8)
    stage_three(2)
    encode(24, 8)
    enc_right = remote(
        enc.at[pl.ds(NODE - HALO_N, HALO_N)], enc.at[pl.ds(NODE, HALO_N)],
        enc_send.at[1], enc_recv.at[1], right)
    stage_three(3)
    for first_at in range(4):
        stage_four(first_at)

    stores = []
    for part in range(4):
        own_rows[part].wait()
        for number in range(15):
            pairs[part, number].wait_recv()
        store = pltpu.make_async_copy(full.at[part], w_all.at[part], store_sem.at[part])
        store.start()
        stores.append(store)
    enc_left.wait_recv()
    enc_right.wait_recv()
    enc_out[...] = enc[...]
    for copy in sent:
        copy.wait_send()
    for store in stores:
        store.wait()


def gather_and_encode(fields, cell_index, interp_weight, w_qkv, w_out):
    vmem = pl.BlockSpec(memory_space=pltpu.VMEM)
    anywhere = pl.BlockSpec(memory_space=pl.ANY)
    dma = pltpu.SemaphoreType.DMA
    return pl.pallas_call(
        comm_kernel,
        out_shape=(
            jax.ShapeDtypeStruct((2 * NODE, LANES), jnp.bfloat16),
            jax.ShapeDtypeStruct((4, 1024, 1024), jnp.bfloat16),
        ),
        in_specs=[anywhere, pl.BlockSpec(memory_space=pltpu.SMEM), vmem, anywhere, anywhere],
        out_specs=(vmem, anywhere),
        scratch_shapes=[
            pltpu.VMEM((CH, REACH), jnp.bfloat16),
            pltpu.VMEM((REACH, LANES), jnp.float32),
            pltpu.VMEM((BLK * LANES, LANES), jnp.float32),
            pltpu.VMEM((2 * NODE, LANES), jnp.bfloat16),
            pltpu.VMEM((4, 1024, 1024), jnp.bfloat16),
            dma((5,)), dma((2,)), dma((2,)), dma((2,)), dma((2,)),
            dma((60,)), dma((60,)), dma((60,)), dma((60,)), dma((4,)),
        ],
        compiler_params=pltpu.CompilerParams(
            collective_id=0, has_side_effects=True, vmem_limit_bytes=40 * 1024 * 1024),
        name="gather_encode",
    )(fields, cell_index, interp_weight, w_qkv, w_out)


def main_kernel(
    enc, w_in, gain, w_all,
    latent, update,
    w_pad, weights, normed, queries, keys, values, attended, load_sem,
):
    f32, bf16 = jnp.float32, jnp.bfloat16
    loads = [
        pltpu.make_async_copy(w_all.at[part], weights.at[part], load_sem.at[part])
        for part in range(4)
    ]
    for load in loads:
        load.start()
    w_pad[...] = jnp.zeros_like(w_pad)
    w_pad[0:CH, :] = w_in[...]

    def embed(chunk, keep):
        rows = pl.ds(pl.multiple_of(chunk * 128, 128), 128)
        embedded = jnp.dot(enc[rows, :], w_pad[...], preferred_element_type=f32)
        if keep:
            latent[rows, :] = embedded.astype(bf16)
        average = jnp.mean(embedded, axis=1, keepdims=True)
        centered = embedded - average
        spread = jnp.mean(centered * centered, axis=1, keepdims=True)
        normed[rows, :] = (centered * lax.rsqrt(spread + 1e-05) * gain[...]).astype(bf16)

    @pl.loop(0, 4)
    def _(chunk):
        embed(chunk, True)

    @pl.loop(4, 8)
    def _(chunk):
        embed(chunk, False)

    wide = 256
    row_head = lax.broadcasted_iota(jnp.int32, (wide, wide), 0) // 64
    col_head = lax.broadcasted_iota(jnp.int32, (wide, wide), 1) // 64
    same_head = jnp.where(row_head == col_head, 1.0, 0.0).astype(bf16)

    def unit(projected, factor):
        squares = projected * projected
        high = squares.astype(bf16)
        low = (squares - high.astype(f32)).astype(bf16)
        total = jnp.dot(high, same_head, preferred_element_type=f32) + jnp.dot(
            low, same_head, preferred_element_type=f32)
        return (projected * (lax.rsqrt(total * (1.0 / 64) + 1e-06) * factor)).astype(bf16)

    for load in loads[:3]:
        load.wait()

    @pl.loop(0, 4)
    def _(group):
        cols = pl.ds(pl.multiple_of(group * wide, wide), wide)
        for chunk in range(4):
            rows = slice(chunk * 256, chunk * 256 + 256)
            some = normed[rows, :]
            if chunk < 2:
                queries[rows, cols] = unit(
                    jnp.dot(some, weights[0, :, cols], preferred_element_type=f32),
                    math.log2(math.e) / 8)
            keys[rows, cols] = unit(
                jnp.dot(some, weights[1, :, cols], preferred_element_type=f32), 1.0)
            values[rows, cols] = jnp.dot(
                some, weights[2, :, cols], preferred_element_type=f32).astype(bf16)

    @pl.loop(0, HEADS // 2)
    def _(pair):
        cols = pl.ds(pl.multiple_of(pair * LANES, LANES), LANES)
        key_pair = keys[:, cols]
        value_pair = values[:, cols]
        value_low = lax.broadcasted_iota(jnp.int32, value_pair.shape, 1) < 64
        ones = jnp.ones_like(value_pair)
        value_one = jnp.where(value_low, value_pair, ones)
        value_two = jnp.where(value_low, ones, value_pair)
        for chunk in range(2):
            rows = slice(chunk * 256, chunk * 256 + 256)
            query_pair = queries[rows, cols]
            query_low = lax.broadcasted_iota(jnp.int32, query_pair.shape, 1) < 64
            none = jnp.zeros_like(query_pair)

            def head(query, value):
                scores = lax.dot_general(
                    query, key_pair, (((1,), (1,)), ((), ())), preferred_element_type=f32)
                return jnp.dot(jnp.exp2(scores).astype(bf16), value, preferred_element_type=f32)

            one = head(jnp.where(query_low, query_pair, none), value_one)
            two = head(jnp.where(query_low, none, query_pair), value_two)
            low = lax.broadcasted_iota(jnp.int32, one.shape, 1) < 64
            top = jnp.where(low, one, two)
            total = pltpu.roll(jnp.where(low, two, one), 64, 1)
            attended[rows, cols] = (top / total).astype(bf16)

    loads[3].wait()

    @pl.loop(0, 2)
    def _(chunk):
        rows = pl.ds(pl.multiple_of(chunk * 256, 256), 256)
        update[rows, :] = jnp.dot(
            attended[rows, :], weights[3], preferred_element_type=f32).astype(bf16)


def attend_all(enc, w_in, gain, w_all):
    vmem = pl.BlockSpec(memory_space=pltpu.VMEM)
    bf16 = jnp.bfloat16
    return pl.pallas_call(
        main_kernel,
        out_shape=(jax.ShapeDtypeStruct((NODE, 1024), bf16),) * 2,
        in_specs=[vmem, vmem, vmem, pl.BlockSpec(memory_space=pl.ANY)],
        out_specs=(vmem, vmem),
        scratch_shapes=[
            pltpu.VMEM((LANES, 1024), bf16),
            pltpu.VMEM((4, 1024, 1024), bf16),
            pltpu.VMEM((2 * NODE, 1024), bf16),
            pltpu.VMEM((NODE, 1024), bf16),
            pltpu.VMEM((2 * NODE, 1024), bf16),
            pltpu.VMEM((2 * NODE, 1024), bf16),
            pltpu.VMEM((NODE, 1024), bf16),
            pltpu.SemaphoreType.DMA((4,)),
        ],
        compiler_params=pltpu.CompilerParams(vmem_limit_bytes=48 * 1024 * 1024),
        name="attend_all",
    )(enc, w_in, gain, w_all)


def shards(fields, cell_index, interp_weight, w_in, ln_gain, w_qkv, w_out):
    enc, w_all = gather_and_encode(fields[0], cell_index, interp_weight, w_qkv, w_out)
    latent, update = attend_all(enc, w_in, ln_gain[None], w_all)
    return (latent[None], update[None])


def solution(mesh):
    placed = (
        P("dp", None, "space"),
        P("space", None),
        P("space", None, None),
        P(),
        P(),
        P("dp", None),
        P("dp", None),
    )
    return jax.shard_map(
        shards,
        mesh=mesh,
        in_specs=placed,
        out_specs=(P("dp", "space", None), P("dp", "space", None)),
        check_vma=False,
    )
```

time: 251 us -> 99.3 us (0.40)
  the two profiles are of different devices: /device:TPU:192 before, /device:TPU:26 now
where the time goes in v1:
time: 99.3 us; the launch traced here: 99 us
  Pallas kernels  88.8 us (89%)
  local copies, waits for them, and re-layouts  9.51 us (10%)
    pallas_call x1, Pallas kernels, gather_and_encode(): pl.pallas_call(comm_kernel, out_shape=(jax.ShapeDtypeStruct((2 * NODE, LA...  61.8 us
    pallas_call x1, Pallas kernels, attend_all(): pl.pallas_call(main_kernel, out_shape=(jax.ShapeDtypeStruct((NODE, 1024),...  27.1 us
    unnamed x16, local copies, waits for them, and re-layouts  9.51 us

profile of v1, /device:TPU:26, one launch (start us, length us, event | category | flops | bytes accessed | tf_op | source)
XLA Modules:
  0.0 99.0 jit_solution(7504654016093307039)
XLA Ops:
  0.6 0.0 copy-start.1
  0.6 1.1 %copy-done.1 = bf16[1,100,4096]{2,1,0:T(8,128)(2,1)S(1)} copy-done((bf16[1,100,4096]{2,1,0:T(8,128)(2,1)S(1)}, bf16[1,100,4096]{2,1,0:T(8,128)(2,1)}, u32[]{:S(2)}) %copy-start.1) | copy-done | bytes 819224
  1.8 0.0 copy-start.2
  1.8 1.0 %copy-done.2 = bf16[64,3072]{1,0:T(8,128)(2,1)S(1)} copy-done((bf16[64,3072]{1,0:T(8,128)(2,1)S(1)}, bf16[64,3072]{1,0:T(8,128)(2,1)}, u32[]{:S(2)}) %copy-start.2) | copy-done | bytes 393240
  2.8 0.0 copy-start.4
  2.8 0.9 copy-done.4
  3.7 0.0 copy-start.5
  3.7 0.9 copy-done.5
  4.6 0.0 copy-start.6
  4.6 0.7 copy-done.6
  5.3 61.8 %gather_encode.1 = (bf16[1024,128]{1,0:T(8,128)(2,1)S(1)}, bf16[4,1024,1024]{2,1,0:T(8,128)(2,1)S(1)}) custom-call(bf16[100,4096]{1,0:T(8,128)(2,1)S(1)} %bitcast.4, s32[32,128]{1,0:T(8,128)S(1)} %copy-done.6, bf16[32,16,128]{2,1,0:T(8,128)(2,1)S(1)} %copy-done.4, bf16[64,3072]{1,0:T(8,128)(2,1)S(1)} %copy-done.2, bf16[64,1024]{1,0:T(8,128)(2,1)S(1)} %copy-done.5), custom_call_target="tpu_custom_call" | custom-call | tf_op jit(solution)/shard_map/gather_encode/pallas_call | solution.py:243
  67.1 0.0 copy-start
  67.1 3.2 %copy-done = bf16[4,1024,1024]{2,1,0:T(8,128)(2,1)} copy-done((bf16[4,1024,1024]{2,1,0:T(8,128)(2,1)}, bf16[4,1024,1024]{2,1,0:T(8,128)(2,1)S(1)}, u32[]{:S(2)}) %copy-start) | copy-done | bytes 8388632
  70.3 0.0 copy-start.3
  70.3 0.9 copy-done.3
  71.2 0.0 copy-start.7
  71.2 0.7 copy-done.7
  71.9 27.1 %attend_all.1 = (bf16[512,1024]{1,0:T(8,128)(2,1)}, bf16[512,1024]{1,0:T(8,128)(2,1)}) custom-call(bf16[1024,128]{1,0:T(8,128)(2,1)S(1)} %get-tuple-element.6.enc, bf16[100,1024]{1,0:T(8,128)(2,1)S(1)} %copy-done.3, f32[1,1024]{1,0:T(1,128)S(1)} %bitcast.5, bf16[4,1024,1024]{2,1,0:T(8,128)(2,1)} %copy-done), custom_call_target="tpu_custom_call" | custom-call | tf_op jit(solution)/shard_map/attend_all/pallas_call | solution.py:369
Async XLA Ops:
  0.6 1.2 %copy-start.1 = (bf16[1,100,4096]{2,1,0:T(8,128)(2,1)S(1)}, bf16[1,100,4096]{2,1,0:T(8,128)(2,1)}, u32[]{:S(2)}) copy-start(bf16[1,100,4096]{2,1,0:T(8,128)(2,1)} %param.7) | copy-start | bytes 2457604
  1.8 1.0 %copy-start.2 = (bf16[64,3072]{1,0:T(8,128)(2,1)S(1)}, bf16[64,3072]{1,0:T(8,128)(2,1)}, u32[]{:S(2)}) copy-start(bf16[64,3072]{1,0:T(8,128)(2,1)} %w_qkv.1) | copy-start | bytes 1179652
  2.8 0.9 copy-start.4
  3.7 0.9 copy-start.5
  4.6 0.7 copy-start.6
  67.1 3.2 %copy-start = (bf16[4,1024,1024]{2,1,0:T(8,128)(2,1)}, bf16[4,1024,1024]{2,1,0:T(8,128)(2,1)S(1)}, u32[]{:S(2)}) copy-start(bf16[4,1024,1024]{2,1,0:T(8,128)(2,1)S(1)} %get-tuple-element.7.w_all) | copy-start | bytes 25165828
  70.3 0.9 copy-start.3
  71.2 0.7 copy-start.7

commit v2 on v0

v2 whole, which is shorter than its diff:
```python
import math

import jax
import jax.numpy as jnp
from jax import lax
from jax.experimental import pallas as pl
from jax.experimental.pallas import tpu as pltpu
from jax.sharding import PartitionSpec as P

HEADS = 16
CH = 100
HALO_C = 1024
HALO_N = 256
NODE = 512
BLK = 32
CELL = 4096
REACH = CELL + 2 * HALO_C
LANES = 128
SHARD = 64
SLAB = 512
WIDE = 256
MESH = pl.DeviceIdType.MESH
F32, BF16 = jnp.float32, jnp.bfloat16
Q, K, V, O = 0, 1, 2, 3
FIRST = {Q: "x", K: "y", V: "y", O: "x"}
ORDER = (K, Q, V)
RELATIVE = (0, -1, 1, 2)


def everything(
    fields, index_hbm, weight_hbm, w_in_hbm, gain_hbm, w_qkv, w_out,
    latent_hbm, update_hbm,
    index, weight, w_in, gain, ext, ext_t, picked, enc, full,
    w_pad, normed, raw, queries, keys, values, attended, latent, update,
    local_sem, own_sem, cell_send, cell_recv, enc_send, enc_recv,
    plane_send, plane_recv, pair_send, pair_recv,
):
    dp = lax.axis_index("dp")
    sp = lax.axis_index("space")
    x, y = dp % 4, dp // 4
    core, side, z = sp % 2, (sp // 2) % 2, sp // 4

    def at(new_y, new_x, new_z, new_side, new_core):
        return (new_y * 4 + new_x, new_z * 4 + new_side * 2 + new_core)

    up_side = (side + (y + 1) // 4) % 2
    down_side = (side + 1 - (y + 3) // 4) % 2
    step_to = {
        ("x", 1): at(y, (x + 1) % 4, z, side, core),
        ("x", -1): at(y, (x + 3) % 4, z, side, core),
        ("y", 1): at((y + 1) % 4, x, z, up_side, core),
        ("y", -1): at((y + 3) % 4, x, z, down_side, core),
    }
    partner = at(y, x, z, side, 1 - core)
    left = (dp, (sp + 31) % 32)
    right = (dp, (sp + 1) % 32)
    far = (dp, (sp + 31 + 2 * core) % 32)

    own_cells = pltpu.make_async_copy(fields, ext.at[:, pl.ds(HALO_C, CELL)], local_sem.at[0])
    own_cells.start()
    small = [
        pltpu.make_async_copy(source, place, local_sem.at[1 + i])
        for i, (source, place) in enumerate(
            ((index_hbm, index), (weight_hbm, weight), (w_in_hbm, w_in), (gain_hbm, gain)))
    ]
    for copy in small:
        copy.start()

    def shard(part, half):
        if part == O:
            return w_out.at[:, pl.ds(pl.multiple_of(half * SLAB, SLAB), SLAB)]
        return w_qkv.at[:, pl.ds(pl.multiple_of(part * 1024 + half * SLAB, SLAB), SLAB)]

    own_rows = {}
    for part in (K, Q, V, O):
        for half in range(2):
            own_rows[part, half] = pltpu.make_async_copy(
                shard(part, half),
                full.at[2 * part + half, pl.ds(pl.multiple_of(dp * SHARD, SHARD), SHARD)],
                own_sem.at[2 * part + half])
            own_rows[part, half].start()

    barrier = pltpu.get_barrier_semaphore()
    for other in list(step_to.values()) + [partner, far]:
        pl.semaphore_signal(barrier, inc=1, device_id=other, device_id_type=MESH)
    pl.semaphore_wait(barrier, 6)

    sent = []

    def remote(src, dst, s_sem, r_sem, target):
        copy = pltpu.make_async_remote_copy(
            src_ref=src, dst_ref=dst, send_sem=s_sem, recv_sem=r_sem,
            device_id=target, device_id_type=MESH,
        )
        copy.start()
        sent.append(copy)
        return copy

    def place(part, first, second, begin=0, size=SHARD):
        if FIRST[part] == "x":
            piece_y, piece_x = (y + 4 + second) % 4, (x + 4 + first) % 4
        else:
            piece_y, piece_x = (y + 4 + first) % 4, (x + 4 + second) % 4
        start = pl.multiple_of((piece_y * 4 + piece_x) * SHARD + begin, 32)
        return full.at[2 * part + core, pl.ds(start, size)]

    plane, pairs = {}, {}

    def move(part, first, second, axis, direction, number, begin=0, size=SHARD):
        target = place(part, first, second, begin, size)
        source = target
        if first == 0 and second == 0:
            source = shard(part, core)
        plane[part, number] = remote(
            source, target, plane_send.at[part * 20 + number], plane_recv.at[part * 20 + number],
            step_to[axis, direction])

    def second_axis(part):
        return "y" if FIRST[part] == "x" else "x"

    def hand_on(part, first, second, unit):
        here = place(part, first, second)
        number = part * 15 + unit
        pairs[part, unit] = remote(here, here, pair_send.at[number], pair_recv.at[number], partner)

    def outward(part, first_at):
        for kind, direction in ((0, 1), (1, -1)):
            move(part, RELATIVE[first_at], 0, second_axis(part), direction, 4 + 4 * first_at + kind)

    def begin(parts):
        for part in parts:
            move(part, 0, 0, FIRST[part], 1, 0)
            move(part, 0, 0, FIRST[part], -1, 1)
        for part in parts:
            outward(part, 0)

    cells_right = remote(
        fields.at[:, pl.ds(CELL - HALO_C, HALO_C)], ext.at[:, pl.ds(0, HALO_C)],
        cell_send.at[0], cell_recv.at[0], right)
    cells_left = remote(
        fields.at[:, pl.ds(0, HALO_C)], ext.at[:, pl.ds(HALO_C + CELL, HALO_C)],
        cell_send.at[1], cell_recv.at[1], left)
    begin(ORDER)

    def stage_one(part):
        for kind, relative, direction, begin in ((0, -1, 1, 0), (1, 1, -1, 32)):
            plane[part, kind].wait_recv()
            move(part, relative, 0, FIRST[part], direction, 2 + kind, begin, 32)
            outward(part, 1 + kind)
            hand_on(part, relative, 0, kind)

    def stage_two(part):
        plane[part, 2].wait_recv()
        plane[part, 3].wait_recv()
        outward(part, 3)
        hand_on(part, 2, 0, 2)

    def stage_three(part, first_at):
        for kind, relative, direction, begin in ((0, -1, 1, 0), (1, 1, -1, 32)):
            number = 4 + 4 * first_at
            plane[part, number + kind].wait_recv()
            move(part, RELATIVE[first_at], relative, second_axis(part), direction,
                 number + 2 + kind, begin, 32)
            hand_on(part, RELATIVE[first_at], relative, 3 + 3 * first_at + kind)

    def stage_four(part, first_at):
        number = 4 + 4 * first_at
        plane[part, number + 2].wait_recv()
        plane[part, number + 3].wait_recv()
        hand_on(part, RELATIVE[first_at], 2, 3 + 3 * first_at + 2)

    def finish(part):
        for half in range(2):
            own_rows[part, half].wait()
        for unit in range(15):
            pairs[part, unit].wait_recv()

    def turn(start, count):
        @pl.loop(0, count // 4)
        def _(i):
            for k in range(4):
                at_cell = pl.multiple_of(start + i * (4 * LANES) + k * LANES, LANES)
                ext_t[pl.ds(at_cell, LANES), 0:CH] = ext[:, pl.ds(at_cell, LANES)].astype(F32).T

    def encode(first_block, count):
        @pl.loop(first_block, first_block + count)
        def _(b):
            base = pl.multiple_of(b * LANES, LANES)
            for j in range(LANES):
                picked[pl.ds(base + j, 1), :] = ext_t[pl.ds(index[b, j], 1), :]
        for b in range(first_block, first_block + count):
            rows = picked[b * LANES:(b + 1) * LANES, :].astype(BF16)
            mixed = jnp.dot(weight[b], rows, preferred_element_type=F32)
            lane = lax.broadcasted_iota(jnp.int32, mixed.shape, 1)
            enc[b * 16:(b + 1) * 16, :] = jnp.where(lane < CH, mixed, 0.0).astype(BF16)

    def embed(chunk, keep):
        rows = slice(chunk * 128, chunk * 128 + 128)
        embedded = jnp.dot(enc[rows, :], w_pad[...], preferred_element_type=F32)
        if keep:
            latent[rows, :] = embedded.astype(BF16)
        average = jnp.mean(embedded, axis=1, keepdims=True)
        centered = embedded - average
        spread = jnp.mean(centered * centered, axis=1, keepdims=True)
        normed[rows, :] = (centered * lax.rsqrt(spread + 1e-05) * gain[...]).astype(BF16)

    row_head = lax.broadcasted_iota(jnp.int32, (WIDE, WIDE), 0) // 64
    col_head = lax.broadcasted_iota(jnp.int32, (WIDE, WIDE), 1) // 64
    same_head = jnp.where(row_head == col_head, 1.0, 0.0).astype(BF16)

    def unit_rows(projected, factor):
        squares = (projected * projected).astype(BF16)
        total = jnp.dot(squares, same_head, preferred_element_type=F32)
        return (projected * (lax.rsqrt(total * (1.0 / 64) + 1e-06) * factor)).astype(BF16)

    def project(part):
        @pl.loop(0, 4)
        def _(group):
            cols = pl.ds(pl.multiple_of(group * WIDE, WIDE), WIDE)
            block = full[2 * part + group // 2, :, pl.ds(pl.multiple_of((group % 2) * WIDE, WIDE), WIDE)]
            for chunk in range(2 if part == Q else 4):
                rows = slice(chunk * 256, chunk * 256 + 256)
                projected = jnp.dot(normed[rows, :], block, preferred_element_type=F32)
                if part == V:
                    values[rows, cols] = projected.astype(BF16)
                else:
                    raw[rows, cols] = projected
        if part == V:
            return

        @pl.loop(0, 4)
        def _(group):
            cols = pl.ds(pl.multiple_of(group * WIDE, WIDE), WIDE)
            for chunk in range(2 if part == Q else 4):
                rows = slice(chunk * 256, chunk * 256 + 256)
                if part == Q:
                    queries[rows, cols] = unit_rows(raw[rows, cols], math.log2(math.e) / 8)
                else:
                    keys[rows, cols] = unit_rows(raw[rows, cols], 1.0)

    own_cells.wait()
    for copy in small:
        copy.wait()
    w_pad[...] = jnp.zeros_like(w_pad)
    w_pad[0:CH, :] = w_in[...]
    turn(HALO_C, CELL // LANES)
    stage_one(Q)
    cells_right.wait_recv()
    turn(0, HALO_C // LANES)
    cells_left.wait_recv()
    turn(HALO_C + CELL, HALO_C // LANES)
    encode(0, 8)
    stage_two(Q)
    encode(8, 8)
    enc_left = remote(
        enc.at[pl.ds(0, HALO_N)], enc.at[pl.ds(NODE + HALO_N, HALO_N)],
        enc_send.at[0], enc_recv.at[0], left)
    stage_one(K)
    encode(16, 8)
    stage_one(V)
    encode(24, 8)
    enc_right = remote(
        enc.at[pl.ds(NODE - HALO_N, HALO_N)], enc.at[pl.ds(NODE, HALO_N)],
        enc_send.at[1], enc_recv.at[1], right)
    embed(0, True)
    embed(1, True)
    stage_two(K)
    embed(2, True)
    stage_two(V)
    embed(3, True)
    latent_out = pltpu.make_async_copy(latent, latent_hbm, local_sem.at[5])
    latent_out.start()
    for quarter in range(4):
        for part in ORDER:
            stage_three(part, quarter)
    enc_left.wait_recv()
    enc_right.wait_recv()
    for quarter in range(4):
        embed(4 + quarter, False)
        for part in ORDER:
            stage_four(part, quarter)
    begin((O,))
    finish(K)
    project(K)
    stage_one(O)
    finish(Q)
    project(Q)
    stage_two(O)
    finish(V)
    project(V)
    for quarter in range(4):
        stage_three(O, quarter)

    def attend(pair):
        cols = pl.ds(pl.multiple_of(pair * LANES, LANES), LANES)
        key_pair = keys[:, cols]
        value_pair = values[:, cols]
        value_low = lax.broadcasted_iota(jnp.int32, value_pair.shape, 1) < 64
        ones = jnp.ones_like(value_pair)
        value_one = jnp.where(value_low, value_pair, ones)
        value_two = jnp.where(value_low, ones, value_pair)
        for chunk in range(2):
            rows = slice(chunk * 256, chunk * 256 + 256)
            query_pair = queries[rows, cols]
            query_low = lax.broadcasted_iota(jnp.int32, query_pair.shape, 1) < 64
            none = jnp.zeros_like(query_pair)

            def head(query, value):
                scores = lax.dot_general(
                    query, key_pair, (((1,), (1,)), ((), ())), preferred_element_type=F32)
                return jnp.dot(jnp.exp2(scores).astype(BF16), value, preferred_element_type=F32)

            one = head(jnp.where(query_low, query_pair, none), value_one)
            two = head(jnp.where(query_low, none, query_pair), value_two)
            low = lax.broadcasted_iota(jnp.int32, one.shape, 1) < 64
            top = jnp.where(low, one, two)
            total = pltpu.roll(jnp.where(low, two, one), 64, 1)
            attended[rows, cols] = (top / total).astype(BF16)

    @pl.loop(0, HEADS // 4)
    def _(pair):
        attend(pair)

    for quarter in range(4):
        stage_four(O, quarter)

    @pl.loop(HEADS // 4, HEADS // 2)
    def _(pair):
        attend(pair)

    finish(O)
    outs = []
    for chunk in range(2):
        rows = slice(chunk * 256, chunk * 256 + 256)
        for half in range(2):
            update[rows, half * SLAB:(half + 1) * SLAB] = jnp.dot(
                attended[rows, :], full[2 * O + half], preferred_element_type=F32).astype(BF16)
        out = pltpu.make_async_copy(
            update.at[pl.ds(chunk * 256, 256)], update_hbm.at[pl.ds(chunk * 256, 256)],
            local_sem.at[6 + chunk])
        out.start()
        outs.append(out)
    for copy in sent:
        copy.wait_send()
    latent_out.wait()
    for out in outs:
        out.wait()


def shards(fields, cell_index, interp_weight, w_in, ln_gain, w_qkv, w_out):
    hbm = pl.BlockSpec(memory_space=pltpu.MemorySpace.HBM)
    dma = pltpu.SemaphoreType.DMA
    vmem = pltpu.VMEM
    latent, update = pl.pallas_call(
        everything,
        out_shape=(jax.ShapeDtypeStruct((NODE, 1024), BF16),) * 2,
        in_specs=[hbm] * 7,
        out_specs=(hbm, hbm),
        scratch_shapes=[
            pltpu.SMEM((BLK, LANES), jnp.int32),
            vmem((BLK, 16, LANES), BF16),
            vmem((CH, 1024), BF16),
            vmem((1, 1024), F32),
            vmem((CH, REACH), BF16),
            vmem((REACH, LANES), F32),
            vmem((BLK * LANES, LANES), F32),
            vmem((2 * NODE, LANES), BF16),
            vmem((8, 1024, SLAB), BF16),
            vmem((LANES, 1024), BF16),
            vmem((2 * NODE, 1024), BF16),
            vmem((2 * NODE, 1024), F32),
            vmem((NODE, 1024), BF16),
            vmem((2 * NODE, 1024), BF16),
            vmem((2 * NODE, 1024), BF16),
            vmem((NODE, 1024), BF16),
            vmem((NODE, 1024), BF16),
            vmem((NODE, 1024), BF16),
            dma((8,)), dma((8,)), dma((2,)), dma((2,)), dma((2,)), dma((2,)),
            dma((80,)), dma((80,)), dma((60,)), dma((60,)),
        ],
        compiler_params=pltpu.CompilerParams(
            collective_id=0, has_side_effects=True, vmem_limit_bytes=60 * 1024 * 1024),
        name="everything",
    )(fields[0], cell_index, interp_weight, w_in, ln_gain[None], w_qkv, w_out)
    return (latent[None], update[None])


def solution(mesh):
    placed = (
        P("dp", None, "space"),
        P("space", None),
        P("space", None, None),
        P(),
        P(),
        P("dp", None),
        P("dp", None),
    )
    return jax.shard_map(
        shards,
        mesh=mesh,
        in_specs=placed,
        out_specs=(P("dp", "space", None), P("dp", "space", None)),
        check_vma=False,
    )
```

time: 251 us -> 75.2 us (0.30)
  the two profiles are of different devices: /device:TPU:192 before, /device:TPU:1 now
where the time goes in v2:
time: 75.2 us; the launch traced here: 75 us
  Pallas kernels  71.1 us (95%)
  local copies, waits for them, and re-layouts  3.32 us (4%)
    pallas_call x1, Pallas kernels, shards(): pl.pallas_call(everything, out_shape=(jax.ShapeDtypeStruct((NODE, 1024),...  71.1 us
    unnamed x4, local copies, waits for them, and re-layouts  3.32 us

profile of v2, /device:TPU:1, one launch (start us, length us, event | category | flops | bytes accessed | tf_op | source)
XLA Modules:
  0.0 75.0 jit_solution(16977937702484524534)
XLA Ops:
  0.6 71.1 %everything.1 = (bf16[512,1024]{1,0:T(8,128)(2,1)}, bf16[512,1024]{1,0:T(8,128)(2,1)}) custom-call(bf16[100,4096]{1,0:T(8,128)(2,1)} %bitcast.6, s32[32,128]{1,0:T(8,128)} %index_hbm.1, bf16[32,16,128]{2,1,0:T(8,128)(2,1)} %weight_hbm.1, bf16[100,1024]{1,0:T(8,128)(2,1)} %w_in_hbm.1, f32[1,1024]{1,0:T(1,128)} %bitcast.7, bf16[64,3072]{1,0:T(8,128)(2,1)} %w_qkv.1, ...), custom_call_target="tpu_custom_call" | custom-call | tf_op jit(solution)/shard_map/everything/pallas_call | solution.py:354
  71.7 0.0 copy-start
  71.7 2.4 %copy.11 = bf16[1,512,1024]{2,1,0:T(8,128)(2,1)} copy(bf16[1,512,1024]{2,1,0:T(8,128)(2,1)} %bitcast.5) | data formatting | bytes 2097152
  74.1 0.0 copy-done
  74.1 1.0 %copy.12 = bf16[1,512,1024]{2,1,0:T(8,128)(2,1)} copy(bf16[1,512,1024]{2,1,0:T(8,128)(2,1)S(1)} %bitcast.4) | data formatting | bytes 2097152
Async XLA Ops:
  71.7 2.4 %copy-start = (bf16[512,1024]{1,0:T(8,128)(2,1)S(1)}, bf16[512,1024]{1,0:T(8,128)(2,1)}, u32[]{:S(2)}) copy-start(bf16[512,1024]{1,0:T(8,128)(2,1)} %get-tuple-element.5) | copy-start | bytes 3145732

commit v3 on v2

--- a/solution.py
+++ b/solution.py
@@ -22,16 +22,16 @@
 MESH = pl.DeviceIdType.MESH
 F32, BF16 = jnp.float32, jnp.bfloat16
 Q, K, V, O = 0, 1, 2, 3
-FIRST = {Q: "x", K: "y", V: "y", O: "x"}
+FIRST = {Q: "x", K: "y", V: "y", O: "y"}
 ORDER = (K, Q, V)
 RELATIVE = (0, -1, 1, 2)
 
 
 def everything(
     fields, index_hbm, weight_hbm, w_in_hbm, gain_hbm, w_qkv, w_out,
-    latent_hbm, update_hbm,
+    latent, update,
     index, weight, w_in, gain, ext, ext_t, picked, enc, full,
-    w_pad, normed, raw, queries, keys, values, attended, latent, update,
+    w_pad, normed, raw, queries, keys, values, attended,
     local_sem, own_sem, cell_send, cell_recv, enc_send, enc_recv,
     plane_send, plane_recv, pair_send, pair_recv,
 ):
@@ -87,13 +87,14 @@
 
     sent = []
 
-    def remote(src, dst, s_sem, r_sem, target):
+    def remote(src, dst, s_sem, r_sem, target, grouped=False):
         copy = pltpu.make_async_remote_copy(
             src_ref=src, dst_ref=dst, send_sem=s_sem, recv_sem=r_sem,
             device_id=target, device_id_type=MESH,
         )
         copy.start()
-        sent.append(copy)
+        if not grouped:
+            sent.append(copy)
         return copy
 
     def place(part, first, second, begin=0, size=SHARD):
@@ -104,7 +105,7 @@
         start = pl.multiple_of((piece_y * 4 + piece_x) * SHARD + begin, 32)
         return full.at[2 * part + core, pl.ds(start, size)]
 
-    plane, pairs = {}, {}
+    plane = {}
 
     def move(part, first, second, axis, direction, number, begin=0, size=SHARD):
         target = place(part, first, second, begin, size)
@@ -112,16 +113,19 @@
         if first == 0 and second == 0:
             source = shard(part, core)
         plane[part, number] = remote(
-            source, target, plane_send.at[part * 20 + number], plane_recv.at[part * 20 + number],
-            step_to[axis, direction])
+            source, target, plane_send.at[part], plane_recv.at[part * 20 + number],
+            step_to[axis, direction], grouped=True)
 
     def second_axis(part):
         return "y" if FIRST[part] == "x" else "x"
 
     def hand_on(part, first, second, unit):
         here = place(part, first, second)
-        number = part * 15 + unit
-        pairs[part, unit] = remote(here, here, pair_send.at[number], pair_recv.at[number], partner)
+        remote(here, here, pair_send.at[part], pair_recv.at[part], partner, grouped=True)
+
+    def all_pieces(part, sem):
+        rows = full.at[2 * part, pl.ds(0, 15 * SHARD)]
+        pltpu.make_async_copy(rows, rows, sem.at[part]).wait()
 
     def outward(part, first_at):
         for kind, direction in ((0, 1), (1, -1)):
@@ -134,13 +138,17 @@
         for part in parts:
             outward(part, 0)
 
+    for part in (K, V, Q):
+        move(part, 0, 0, FIRST[part], 1, 0)
+        move(part, 0, 0, FIRST[part], -1, 1)
     cells_right = remote(
         fields.at[:, pl.ds(CELL - HALO_C, HALO_C)], ext.at[:, pl.ds(0, HALO_C)],
         cell_send.at[0], cell_recv.at[0], right)
     cells_left = remote(
         fields.at[:, pl.ds(0, HALO_C)], ext.at[:, pl.ds(HALO_C + CELL, HALO_C)],
         cell_send.at[1], cell_recv.at[1], left)
-    begin(ORDER)
+    for part in (K, V, Q):
+        outward(part, 0)
 
     def stage_one(part):
         for kind, relative, direction, begin in ((0, -1, 1, 0), (1, 1, -1, 32)):
@@ -172,8 +180,7 @@
     def finish(part):
         for half in range(2):
             own_rows[part, half].wait()
-        for unit in range(15):
-            pairs[part, unit].wait_recv()
+        all_pieces(part, pair_recv)
 
     def turn(start, count):
         @pl.loop(0, count // 4)
@@ -244,41 +251,38 @@
     w_pad[...] = jnp.zeros_like(w_pad)
     w_pad[0:CH, :] = w_in[...]
     turn(HALO_C, CELL // LANES)
+    stage_one(K)
+    stage_one(V)
     stage_one(Q)
     cells_right.wait_recv()
     turn(0, HALO_C // LANES)
     cells_left.wait_recv()
     turn(HALO_C + CELL, HALO_C // LANES)
     encode(0, 8)
-    stage_two(Q)
+    stage_two(K)
     encode(8, 8)
     enc_left = remote(
         enc.at[pl.ds(0, HALO_N)], enc.at[pl.ds(NODE + HALO_N, HALO_N)],
         enc_send.at[0], enc_recv.at[0], left)
-    stage_one(K)
+    stage_two(V)
     encode(16, 8)
-    stage_one(V)
+    stage_two(Q)
     encode(24, 8)
     enc_right = remote(
         enc.at[pl.ds(NODE - HALO_N, HALO_N)], enc.at[pl.ds(NODE, HALO_N)],
         enc_send.at[1], enc_recv.at[1], right)
-    embed(0, True)
-    embed(1, True)
-    stage_two(K)
-    embed(2, True)
-    stage_two(V)
-    embed(3, True)
-    latent_out = pltpu.make_async_copy(latent, latent_hbm, local_sem.at[5])
-    latent_out.start()
     for quarter in range(4):
+        embed(quarter, True)
         for part in ORDER:
             stage_three(part, quarter)
     enc_left.wait_recv()
     enc_right.wait_recv()
     for quarter in range(4):
+        stage_four(K, quarter)
+    for quarter in range(4):
         embed(4 + quarter, False)
-        for part in ORDER:
-            stage_four(part, quarter)
+        stage_four(Q, quarter)
+        stage_four(V, quarter)
     begin((O,))
     finish(K)
     project(K)
@@ -329,22 +333,16 @@
         attend(pair)
 
     finish(O)
-    outs = []
     for chunk in range(2):
         rows = slice(chunk * 256, chunk * 256 + 256)
         for half in range(2):
             update[rows, half * SLAB:(half + 1) * SLAB] = jnp.dot(
                 attended[rows, :], full[2 * O + half], preferred_element_type=F32).astype(BF16)
-        out = pltpu.make_async_copy(
-            update.at[pl.ds(chunk * 256, 256)], update_hbm.at[pl.ds(chunk * 256, 256)],
-            local_sem.at[6 + chunk])
-        out.start()
-        outs.append(out)
     for copy in sent:
         copy.wait_send()
-    latent_out.wait()
-    for out in outs:
-        out.wait()
+    for part in (Q, K, V, O):
+        all_pieces(part, plane_send)
+        all_pieces(part, pair_send)
 
 
 def shards(fields, cell_index, interp_weight, w_in, ln_gain, w_qkv, w_out):
@@ -355,7 +353,7 @@
         everything,
         out_shape=(jax.ShapeDtypeStruct((NODE, 1024), BF16),) * 2,
         in_specs=[hbm] * 7,
-        out_specs=(hbm, hbm),
+        out_specs=(pl.BlockSpec(memory_space=pltpu.VMEM),) * 2,
         scratch_shapes=[
             pltpu.SMEM((BLK, LANES), jnp.int32),
             vmem((BLK, 16, LANES), BF16),
@@ -373,15 +371,14 @@
             vmem((2 * NODE, 1024), BF16),
             vmem((2 * NODE, 1024), BF16),
             vmem((NODE, 1024), BF16),
-            vmem((NODE, 1024), BF16),
-            vmem((NODE, 1024), BF16),
             dma((8,)), dma((8,)), dma((2,)), dma((2,)), dma((2,)), dma((2,)),
-            dma((80,)), dma((80,)), dma((60,)), dma((60,)),
+            dma((4,)), dma((80,)), dma((4,)), dma((4,)),
         ],
         compiler_params=pltpu.CompilerParams(
-            collective_id=0, has_side_effects=True, vmem_limit_bytes=60 * 1024 * 1024),
+            collective_id=0, has_side_effects=True, vmem_limit_bytes=40 * 1024 * 1024),
         name="everything",
-    )(fields[0], cell_index, interp_weight, w_in, ln_gain[None], w_qkv, w_out)
+    )(*(pltpu.with_memory_space_constraint(array, pltpu.MemorySpace.HBM) for array in (
+        fields[0], cell_index, interp_weight, w_in, ln_gain[None], w_qkv, w_out)))
     return (latent[None], update[None])
 
 

time: 75.2 us -> 71 us (0.944)
  the two profiles are of different devices: /device:TPU:1 before, /device:TPU:8 now
where the time goes in v3:
time: 71 us; the launch traced here: 70.9 us
  Pallas kernels  68.3 us (96%)
  local copies, waits for them, and re-layouts  1.94 us (3%)
    pallas_call x1, Pallas kernels, shards(): pl.pallas_call(everything, out_shape=(jax.ShapeDtypeStruct((NODE, 1024),...  68.3 us
    unnamed x2, local copies, waits for them, and re-layouts  1.94 us

profile of v3, /device:TPU:8, one launch (start us, length us, event | category | flops | bytes accessed | tf_op | source)
XLA Modules:
  0.0 70.9 jit_solution(14148814800419367773)
XLA Ops:
  0.6 68.3 %everything.1 = (bf16[512,1024]{1,0:T(8,128)(2,1)S(1)}, bf16[512,1024]{1,0:T(8,128)(2,1)S(1)}) custom-call(bf16[100,4096]{1,0:T(8,128)(2,1)} %bitcast.6, s32[32,128]{1,0:T(8,128)} %index_hbm.1, bf16[32,16,128]{2,1,0:T(8,128)(2,1)} %weight_hbm.1, bf16[100,1024]{1,0:T(8,128)(2,1)} %w_in_hbm.1, f32[1,1024]{1,0:T(1,128)} %bitcast.7, bf16[64,3072]{1,0:T(8,128)(2,1)} %w_qkv.1, ...), custom_call_target="tpu_custom_call" | custom-call | tf_op jit(solution)/shard_map/everything/pallas_call | solution.py:352
  68.9 1.0 %copy.11 = bf16[1,512,1024]{2,1,0:T(8,128)(2,1)} copy(bf16[1,512,1024]{2,1,0:T(8,128)(2,1)S(1)} %bitcast.5) | data formatting | bytes 2097152
  69.9 1.0 %copy.12 = bf16[1,512,1024]{2,1,0:T(8,128)(2,1)} copy(bf16[1,512,1024]{2,1,0:T(8,128)(2,1)S(1)} %bitcast.4) | data formatting | bytes 2097152

commit v4 on v3

--- a/solution.py
+++ b/solution.py
@@ -138,7 +138,7 @@
         for part in parts:
             outward(part, 0)
 
-    for part in (K, V, Q):
+    for part in (K, V):
         move(part, 0, 0, FIRST[part], 1, 0)
         move(part, 0, 0, FIRST[part], -1, 1)
     cells_right = remote(
@@ -147,8 +147,10 @@
     cells_left = remote(
         fields.at[:, pl.ds(0, HALO_C)], ext.at[:, pl.ds(HALO_C + CELL, HALO_C)],
         cell_send.at[1], cell_recv.at[1], left)
-    for part in (K, V, Q):
-        outward(part, 0)
+    outward(K, 0)
+    outward(V, 0)
+    move(Q, 0, 0, FIRST[Q], 1, 0)
+    move(Q, 0, 0, FIRST[Q], -1, 1)
 
     def stage_one(part):
         for kind, relative, direction, begin in ((0, -1, 1, 0), (1, 1, -1, 32)):
@@ -253,45 +255,57 @@
     turn(HALO_C, CELL // LANES)
     stage_one(K)
     stage_one(V)
-    stage_one(Q)
+    stage_three(K, 0)
+    stage_three(V, 0)
     cells_right.wait_recv()
     turn(0, HALO_C // LANES)
     cells_left.wait_recv()
     turn(HALO_C + CELL, HALO_C // LANES)
     encode(0, 8)
     stage_two(K)
+    stage_three(K, 1)
     encode(8, 8)
     enc_left = remote(
         enc.at[pl.ds(0, HALO_N)], enc.at[pl.ds(NODE + HALO_N, HALO_N)],
         enc_send.at[0], enc_recv.at[0], left)
     stage_two(V)
+    stage_three(V, 1)
     encode(16, 8)
-    stage_two(Q)
+    stage_three(K, 2)
+    stage_three(V, 2)
     encode(24, 8)
     enc_right = remote(
         enc.at[pl.ds(NODE - HALO_N, HALO_N)], enc.at[pl.ds(NODE, HALO_N)],
         enc_send.at[1], enc_recv.at[1], right)
-    for quarter in range(4):
-        embed(quarter, True)
-        for part in ORDER:
-            stage_three(part, quarter)
+    outward(Q, 0)
+    stage_one(Q)
+    embed(0, True)
+    embed(1, True)
+    stage_three(K, 3)
+    stage_three(V, 3)
+    embed(2, True)
+    stage_two(Q)
+    embed(3, True)
+    for quarter in range(4):
+        stage_four(K, quarter)
     enc_left.wait_recv()
     enc_right.wait_recv()
     for quarter in range(4):
-        stage_four(K, quarter)
-    for quarter in range(4):
         embed(4 + quarter, False)
-        stage_four(Q, quarter)
         stage_four(V, quarter)
+    for quarter in range(4):
+        stage_three(Q, quarter)
     begin((O,))
     finish(K)
     project(K)
+    for quarter in range(4):
+        stage_four(Q, quarter)
     stage_one(O)
+    finish(V)
+    project(V)
+    stage_two(O)
     finish(Q)
     project(Q)
-    stage_two(O)
-    finish(V)
-    project(V)
     for quarter in range(4):
         stage_three(O, quarter)
 

time: 71 us -> 69.2 us (0.975)
  the two profiles are of different devices: /device:TPU:8 before, /device:TPU:24 now
where the time goes in v4:
time: 69.2 us; the launch traced here: 69.1 us
  Pallas kernels  66.5 us (96%)
  local copies, waits for them, and re-layouts  1.94 us (3%)
    pallas_call x1, Pallas kernels, shards(): pl.pallas_call(everything, out_shape=(jax.ShapeDtypeStruct((NODE, 1024),...  66.5 us
    unnamed x2, local copies, waits for them, and re-layouts  1.94 us

profile of v4, /device:TPU:24, one launch (start us, length us, event | category | flops | bytes accessed | tf_op | source)
XLA Modules:
  0.0 69.1 jit_solution(13659645222418993280)
XLA Ops:
  0.6 66.5 %everything.1 = (bf16[512,1024]{1,0:T(8,128)(2,1)S(1)}, bf16[512,1024]{1,0:T(8,128)(2,1)S(1)}) custom-call(bf16[100,4096]{1,0:T(8,128)(2,1)} %bitcast.6, s32[32,128]{1,0:T(8,128)} %index_hbm.1, bf16[32,16,128]{2,1,0:T(8,128)(2,1)} %weight_hbm.1, bf16[100,1024]{1,0:T(8,128)(2,1)} %w_in_hbm.1, f32[1,1024]{1,0:T(1,128)} %bitcast.7, bf16[64,3072]{1,0:T(8,128)(2,1)} %w_qkv.1, ...), custom_call_target="tpu_custom_call" | custom-call | tf_op jit(solution)/shard_map/everything/pallas_call | solution.py:366
  67.2 1.0 %copy.11 = bf16[1,512,1024]{2,1,0:T(8,128)(2,1)} copy(bf16[1,512,1024]{2,1,0:T(8,128)(2,1)S(1)} %bitcast.5) | data formatting | bytes 2097152
  68.1 1.0 %copy.12 = bf16[1,512,1024]{2,1,0:T(8,128)(2,1)} copy(bf16[1,512,1024]{2,1,0:T(8,128)(2,1)S(1)} %bitcast.4) | data formatting | bytes 2097152
